TPU v7x, 32 devices: a whole 2x2x4 slice. The times are simulated.
32 devices in a mesh: gx: 2 (over x), gy: 4 (over y, core), gz: 4 (over z).
Axes of the slice: x: 2, y: 2, z: 4, core: 2. Of those that a mesh axis runs over, the one named last changes fastest.
Arguments:
- features: bfloat16 [256, 4096], P('gz', ('gy', 'gx')), may hold values from -14 to 14, as said below
- tiles: bfloat16 [32, 32, 128, 128], P('gx', 'gy'), may hold values from -0.5 to 0.5
- block_mask: int32 [32, 32], P('gx', 'gy'), may hold values from 0 to 1, as said below
- tile_counts: int32 [32], P('gx'), may hold values from 1 to 32, as said below
- weight: bfloat16 [256, 256], replicated, may hold values from -0.375 to 0.375
- gamma: float32 [256], P('gz'), may hold values from 0.5 to 2
- beta: float32 [256], P('gz'), may hold values from -3 to 3
Outputs:
- normed: bfloat16 [256, 4096], P('gz', ('gx', 'gy'))
Inputs may be any that keep to these rules, and one draw needn't show every extreme that they name: `features`: channels along dimension 0, nodes along dimension 1. `block_mask`: 1 where block row and block column meet in a nonzero block, else 0; the diagonal is 1. tile_counts[r] is the number of ones in row r of block_mask.
All inputs are finite; a program needn't handle non-finite values.
Results may differ from a plain program's by a relative error of at most 0.013.
Values may be sent and summed in bfloat16 or wider, within the bound.
A program may use at most 64 MiB of HBM per device.

v0:
```python
import jax
import jax.numpy as jnp
from jax import lax
from jax.sharding import PartitionSpec as P


def body(features, tiles, block_mask, tile_counts, weight, gamma, beta):
    panel = lax.all_gather(features, "gx", axis=1, tiled=True)
    local_ch = panel.shape[0]
    rows_blk = tiles.shape[0]
    cols_blk = tiles.shape[1]
    tile_len = tiles.shape[2]
    panels = panel.reshape(local_ch, cols_blk, tile_len)
    prods = jnp.einsum("fcn,rcmn->frcm", panels, tiles, preferred_element_type=jnp.float32)
    share = block_mask.astype(jnp.float32) / tile_counts.astype(jnp.float32)[:, None]
    partial_value = jnp.einsum("frcm,rc->frm", prods, share).reshape(local_ch, rows_blk * tile_len)
    summed = lax.psum(partial_value, "gy")
    width = rows_blk * tile_len // lax.axis_size("gy")
    agg = lax.dynamic_slice_in_dim(summed, lax.axis_index("gy") * width, width, 1)
    agg = agg.astype(jnp.bfloat16)
    offset = lax.axis_index("gz") * local_ch
    full = lax.all_gather(agg, "gz", axis=0, tiled=True)
    w_cols = lax.dynamic_slice_in_dim(weight, offset, local_ch, 1)
    z_vals = jnp.einsum("co,cn->on", w_cols, full, preferred_element_type=jnp.float32)
    total = z_vals.shape[1] * lax.axis_size(("gx", "gy"))
    sums, squares = lax.psum(
        (jnp.sum(z_vals, axis=1), jnp.sum(z_vals * z_vals, axis=1)), ("gx", "gy")
    )
    mean = sums / total
    var = squares / total - mean * mean
    centered = z_vals - mean[:, None]
    scaled = gamma[:, None] * centered * lax.rsqrt(var + 1e-05)[:, None] + beta[:, None]
    return jnp.maximum(scaled, 0.0).astype(jnp.bfloat16)


def solution(mesh):
    in_specs = (
        P("gz", ("gy", "gx")),
        P("gx", "gy", None, None),
        P("gx", "gy"),
        P("gx"),
        P(),
        P("gz"),
        P("gz"),
    )
    out_specs = P("gz", ("gx", "gy"))
    return jax.shard_map(body, mesh=mesh, in_specs=in_specs, out_specs=out_specs, check_vma=False)
```

profile of v0, /device:TPU:0, one launch (start us, length us, event | category | flops | bytes accessed | tf_op | source)
XLA Modules:
  0.0 57.3 jit_solution(9171550169248883873)
XLA Ops:
  0.0 0.0 copy-start
  0.0 0.7 %convert_element_type.13 = f32[16]{0:T(128)S(1)} convert(s32[16]{0:T(128)} %param.10) | non-fusion elementwise | flops 16 | bytes 128 | tf_op jit(solution)/shard_map/convert_element_type | solution.py:15
  0.7 0.7 %divide_bitcast_fusion = bf16[16,8,1,1]{0,1,2,3:T(8,128)(2,1)S(1)} fusion(s32[16,8]{0,1:T(8,128)} %param.9, f32[16]{0:T(128)S(1)} %convert_element_type.13), kind=kLoop, calls=%fused_computation.12 | loop fusion | flops 384 | bytes 832 | tf_op jit(solution)/shard_map/div | solution.py:15
  1.4 0.1 copy.12
  1.5 6.1 %all_gather.6 = bf16[64,1024]{1,0:T(8,128)(2,1)S(1)} all-gather(bf16[64,512]{1,0:T(8,128)(2,1)} %param.7), channel_id=1, replica_groups=mesh['gx'=2,'gy'=4,'gz'=4] {'gx'}, dimensions={1}, use_global_device_ids=true | all-gather | bytes 196608 | tf_op jit(solution)/shard_map/all_gather | solution.py:8
  7.6 3.8 %fusion.4 = bf16[64,16,8,128]{3,0,1,2:T(8,128)(2,1)S(1)} fusion(bf16[16,8,128,128]{3,2,1,0:T(8,128)(2,1)} %param.8, bf16[64,8,128,1]{2,1,0,3:T(8,128)(2,1)S(1)} %bitcast.19), kind=kOutput, calls=%fused_computation.4 | convolution fusion | flops 268435456 | bytes 6422528 | tf_op jit(solution)/shard_map/fcn,rcmn->frcm/dot_general | solution.py:14
  11.4 1.4 %fusion = f32[16,1,64,128]{3,1,2,0:T(1,128)S(1)} fusion(bf16[16,8,1,1]{1,2,3,0:T(2,128)(2,1)S(1)} %copy.12, bf16[64,16,8,128]{3,0,1,2:T(8,128)(2,1)S(1)} %fusion.4), kind=kOutput, calls=%fused_computation | convolution fusion | flops 2097152 | bytes 2621696 | tf_op jit(solution)/shard_map/frcm,rc->frm/dot_general | solution.py:16
  12.8 0.0 copy-start.1
  12.8 0.0 copy-start.2
  12.8 0.3 copy.14
  13.2 0.2 copy.28
  13.3 16.7 %all-reduce.2 = bf16[64,2048]{1,0:T(8,128)(2,1)S(1)} all-reduce(f32[64,2048]{1,0:T(8,128)S(1)} %bitcast.18), channel_id=1, replica_groups=mesh['gx'=2,'gy'=4,'gz'=4] {'gy'}, use_global_device_ids=true, to_apply=%region_0.0 | all-reduce | flops 131072 | bytes 786432 | tf_op jit(solution)/shard_map/psum | solution.py:17
  30.1 14.2 %all_gather.7 = bf16[256,512]{1,0:T(8,128)(2,1)S(1)} all-gather(bf16[64,512]{1,0:T(8,128)(2,1)S(1)} %dynamic-slice_convert_fusion), channel_id=1, replica_groups=mesh['gx'=2,'gy'=4,'gz'=4] {'gz'}, dimensions={0}, use_global_device_ids=true | all-gather | bytes 327680 | tf_op jit(solution)/shard_map/all_gather | solution.py:22
  44.3 0.0 copy-done
  44.3 0.4 fusion.11
  44.7 11.8 %all-reduce = (f32[64]{0:T(128)S(1)}, f32[64]{0:T(128)S(1)}) all-reduce(f32[64]{0:T(128)S(1)} %get-tuple-element.6, f32[64]{0:T(128)S(1)} %get-tuple-element.5), channel_id=1, replica_groups=mesh['gx'=2,'gy'=4,'gz'=4] {'gx','gy'}, use_global_device_ids=true, to_apply=%region_4.0 | all-reduce | flops 128 | bytes 1024 | tf_op jit(solution)/shard_map/psum | solution.py:26
  56.5 0.0 copy-done.1
  56.5 0.0 copy-done.2
  56.5 0.7 %maximum_convert_fusion = bf16[64,512]{1,0:T(8,128)(2,1)} fusion(f32[64,512]{1,0:T(8,128)S(1)} %get-tuple-element.11, f32[64]{0:T(128)S(1)} %copy-done.1, f32[64]{0:T(128)S(1)} %get-tuple-element.10, f32[64]{0:T(128)S(1)} %get-tuple-element.9, f32[64]{0:T(128)S(1)} %copy-done.2), kind=kLoop, calls=%fused_computation.7 | loop fusion | flops 196608 | bytes 197632 | tf_op jit(solution)/shard_map/convert_element_type | solution.py:33
  (3 shorter events, 0.0 us)
Async XLA Ops:
  0.0 44.3 %copy-start = (bf16[256,256]{1,0:T(8,128)(2,1)S(1)}, bf16[256,256]{1,0:T(8,128)(2,1)}, u32[]{:S(2)}) copy-start(bf16[256,256]{1,0:T(8,128)(2,1)} %param.11) | copy-start | bytes 393220
  12.8 43.7 %copy-start.1 = (f32[64]{0:T(128)S(1)}, f32[64]{0:T(128)}, u32[]{:S(2)}) copy-start(f32[64]{0:T(128)} %param.13) | copy-start | bytes 772
  12.8 43.7 %copy-start.2 = (f32[64]{0:T(128)S(1)}, f32[64]{0:T(128)}, u32[]{:S(2)}) copy-start(f32[64]{0:T(128)} %param.12) | copy-start | bytes 772
where the time goes:
time: 57.5 us; the launch traced here: 57.3 us
  blocking collectives  48.9 us (85%)
  matrix products  5.54 us (10%)
  other arithmetic  2.13 us (4%)
  local copies, waits for them, and re-layouts  0.61 us (1%)
    psum x1, blocking collectives, body(): summed = lax.psum(partial_value, 'gy')  16.7 us
    all_gather x1, blocking collectives, body(): full = lax.all_gather(agg, 'gz', axis=0, tiled=True)  14.2 us
    psum x1, blocking collectives, body(): lax.psum((jnp.sum(z_vals, axis=1), jnp.sum(z_vals * z_vals, axis=1)), ('g...  11.8 us
    all_gather x1, blocking collectives, body(): panel = lax.all_gather(features, 'gx', axis=1, tiled=True)  6.13 us
    dot_general x1, matrix products, body(): jnp.einsum('fcn,rcmn->frcm', panels, tiles, preferred_element_type=jnp.fl...  3.75 us
    dot_general x1, matrix products, body(): jnp.einsum('frcm,rc->frm', prods, share)  1.42 us

commit v1 on v0

--- a/solution.py
+++ b/solution.py
@@ -14,7 +14,7 @@
     prods = jnp.einsum("fcn,rcmn->frcm", panels, tiles, preferred_element_type=jnp.float32)
     share = block_mask.astype(jnp.float32) / tile_counts.astype(jnp.float32)[:, None]
     partial_value = jnp.einsum("frcm,rc->frm", prods, share).reshape(local_ch, rows_blk * tile_len)
-    summed = lax.psum(partial_value, "gy")
+    summed = jnp.sum(lax.all_gather(partial_value, "gy"), 0)
     width = rows_blk * tile_len // lax.axis_size("gy")
     agg = lax.dynamic_slice_in_dim(summed, lax.axis_index("gy") * width, width, 1)
     agg = agg.astype(jnp.bfloat16)

time: 57.5 us -> 80.8 us (1.41)
  waiting for transfers between devices: 0 us -> 24.5 us
  blocking collectives: 48.9 us -> 31.9 us
  between operations: 0.07 us -> 13.4 us
  other arithmetic: 2.13 us -> 3.92 us
    all_gather x0 -> x1, waiting for transfers between devices: none -> 24.4 us  [body(): summed = jnp.sum(lax.all_gather(partial_value, 'gy'), 0)]
    psum x1 -> x0, blocking collectives: 16.7 us -> none  [body(): summed = lax.psum(partial_value, 'gy')]
    reduce_sum x0 -> x1, other arithmetic: none -> 1.79 us  [body(): summed = jnp.sum(lax.all_gather(partial_value, 'gy'), 0)]
    another operation x0 -> x1, local copies, waits for them, and re-layouts: none -> 0.88 us  [body(): summed = jnp.sum(lax.all_gather(partial_value, 'gy'), 0)]
  transfers between devices with their start and end apart: 0 -> 1, of which waited for: 0 -> 1; matrix products, arithmetic and copies ran while one was open for 0% -> 0% of each run, Pallas kernels for 0% -> 0%
where the time goes in v1:
time: 80.8 us; the launch traced here: 80.6 us
  blocking collectives  31.9 us (39%)
  waiting for transfers between devices  24.5 us (30%)
  between operations  13.4 us (17%)
  matrix products  5.54 us (7%)
  other arithmetic  3.92 us (5%)
  local copies, waits for them, and re-layouts  1.33 us (2%)
    all_gather x1, waiting for transfers between devices, body(): summed = jnp.sum(lax.all_gather(partial_value, 'gy'), 0)  24.4 us
    all_gather x1, blocking collectives, body(): full = lax.all_gather(agg, 'gz', axis=0, tiled=True)  13.9 us
    psum x1, blocking collectives, body(): lax.psum((jnp.sum(z_vals, axis=1), jnp.sum(z_vals * z_vals, axis=1)), ('g...  11.8 us
    all_gather x1, blocking collectives, body(): panel = lax.all_gather(features, 'gx', axis=1, tiled=True)  6.13 us
    dot_general x1, matrix products, body(): jnp.einsum('fcn,rcmn->frcm', panels, tiles, preferred_element_type=jnp.fl...  3.75 us
    reduce_sum x1, other arithmetic, body(): summed = jnp.sum(lax.all_gather(partial_value, 'gy'), 0)  1.79 us
  transfers between devices with their start and end apart: 1, of which 1 were waited for; matrix products, arithmetic and copies ran while one was open for 0% of the time, Pallas kernels for 0%

profile of v1, /device:TPU:0, one launch (start us, length us, event | category | flops | bytes accessed | tf_op | source)
XLA Modules:
  0.0 80.6 jit_solution(9903522646537438841)
XLA Ops:
  6.5 0.0 copy-start
  6.5 0.0 all-gather.2.cloned.1.call-start
  6.5 0.7 convert_element_type.13
  7.2 0.7 divide_bitcast_fusion
  7.9 0.1 copy.12
  8.0 6.1 %all_gather.9 = bf16[64,1024]{1,0:T(8,128)(2,1)S(1)} all-gather(bf16[64,512]{1,0:T(8,128)(2,1)} %param.7), channel_id=1, replica_groups=mesh['gx'=2,'gy'=4,'gz'=4] {'gx'}, dimensions={1}, use_global_device_ids=true | all-gather | bytes 196608 | tf_op jit(solution)/shard_map/all_gather | solution.py:8
  14.2 3.8 %fusion.4 = bf16[64,16,8,128]{3,0,1,2:T(8,128)(2,1)S(1)} fusion(bf16[16,8,128,128]{3,2,1,0:T(8,128)(2,1)} %param.8, bf16[64,8,128,1]{2,1,0,3:T(8,128)(2,1)S(1)} %bitcast.16), kind=kOutput, calls=%fused_computation.4 | convolution fusion | flops 268435456 | bytes 6422528 | tf_op jit(solution)/shard_map/fcn,rcmn->frcm/dot_general | solution.py:14
  17.9 1.4 %fusion = f32[16,1,64,128]{3,1,2,0:T(1,128)S(1)} fusion(bf16[16,8,1,1]{1,2,3,0:T(2,128)(2,1)S(1)} %copy.12, bf16[64,16,8,128]{3,0,1,2:T(8,128)(2,1)S(1)} %fusion.4), kind=kOutput, calls=%fused_computation | convolution fusion | flops 2097152 | bytes 2621696 | tf_op jit(solution)/shard_map/frcm,rc->frm/dot_general | solution.py:16
  19.4 0.3 copy.27
  19.7 0.9 %all_gather_reshape.3 = f32[1,64,2048]{2,1,0:T(8,128)} reshape(f32[64,16,128]{2,1,0:T(8,128)S(1)} %bitcast.15) | data formatting | bytes 1048576 | tf_op jit(solution)/shard_map/all_gather;reshape | solution.py:17
  20.5 0.0 copy-start.1
  20.6 0.0 copy-start.2
  20.6 0.0 all-gather.2.cloned.1.call-update
  20.6 24.4 %all-gather.2.cloned.1.call-done = f32[4,64,2048]{2,1,0:T(8,128)} async-done(((f32[1,64,2048]{2,1,0:T(8,128)}), f32[4,64,2048]{2,1,0:T(8,128)}) %all-gather.2.cloned.1.call-update) | async-done | bytes 2097168 | tf_op jit(solution)/shard_map/all_gather | solution.py:17
  45.0 1.8 %reduce_sum.27 = bf16[64,2048]{1,0:T(8,128)(2,1)S(1)} reduce(f32[4,64,2048]{2,1,0:T(8,128)} %all-gather.2.cloned.1.call-done, f32[]{:T(128)} %constant.8.clone.1), dimensions={0}, to_apply=%region_0.0 | reduce | flops 393216 | bytes 2359300 | tf_op jit(solution)/shard_map/reduce_sum | solution.py:17
  46.8 13.9 %all_gather.11 = bf16[256,512]{1,0:T(8,128)(2,1)S(1)} all-gather(bf16[64,512]{1,0:T(8,128)(2,1)S(1)} %dynamic-slice_convert_fusion), channel_id=1, replica_groups=mesh['gx'=2,'gy'=4,'gz'=4] {'gz'}, dimensions={0}, use_global_device_ids=true | all-gather | bytes 327680 | tf_op jit(solution)/shard_map/all_gather | solution.py:22
  60.8 0.0 copy-done
  60.8 0.4 fusion.11
  61.1 11.8 %all-reduce = (f32[64]{0:T(128)S(1)}, f32[64]{0:T(128)S(1)}) all-reduce(f32[64]{0:T(128)S(1)} %get-tuple-element.6, f32[64]{0:T(128)S(1)} %get-tuple-element.5), channel_id=1, replica_groups=mesh['gx'=2,'gy'=4,'gz'=4] {'gx','gy'}, use_global_device_ids=true, to_apply=%region_4.0 | all-reduce | flops 128 | bytes 1024 | tf_op jit(solution)/shard_map/psum | solution.py:26
  73.0 0.0 copy-done.1
  73.0 0.0 copy-done.2
  73.0 0.7 maximum_convert_fusion
  (3 shorter events, 0.0 us)
Async XLA Ops:
  6.5 54.2 %copy-start = (bf16[256,256]{1,0:T(8,128)(2,1)S(1)}, bf16[256,256]{1,0:T(8,128)(2,1)}, u32[]{:S(2)}) copy-start(bf16[256,256]{1,0:T(8,128)(2,1)} %param.11) | copy-start | bytes 393220
  6.5 38.5 %all-gather.2.cloned.1.call-start = ((), (), s32[]{:S(2)}) async-start(), calls=%async_computation | async-start | bytes 2621440 | tf_op jit(solution)/shard_map/all_gather | solution.py:17
  20.5 52.4 %copy-start.1 = (f32[64]{0:T(128)S(1)}, f32[64]{0:T(128)}, u32[]{:S(2)}) copy-start(f32[64]{0:T(128)} %param.13) | copy-start | bytes 772
  20.6 52.4 %copy-start.2 = (f32[64]{0:T(128)S(1)}, f32[64]{0:T(128)}, u32[]{:S(2)}) copy-start(f32[64]{0:T(128)} %param.12) | copy-start | bytes 772
Sparse Core Ops, SparseCore 0:
  20.7 24.2 all-gather.1
